TPU v7x, 32 devices: a whole 2x2x4 slice. The times are simulated.
32 devices in a mesh: grp: 4 (over y, core), dev: 8 (over z, x).
Axes of the slice: x: 2, y: 2, z: 4, core: 2. Of those that a mesh axis runs over, the one named last changes fastest.
Arguments:
- basis_values: bfloat16 [128, 256, 512], P(('grp', 'dev')), may hold values from -1 to 1
- stored_density_blocks: bfloat16 [64, 128, 128], P('dev'), may hold values from -0.5 to 0.5
- device_request: int32 [32, 8, 8], P(('grp', 'dev')), may hold values from -1 to 7, as said below
- batch_blocks: int32 [128, 16], P(('grp', 'dev')), may hold values from 0 to 63, as said below
- batch_atom: int32 [128], P(('grp', 'dev')), may hold values from 0 to 999
- point_offset: float32 [3, 128, 256], P(None, ('grp', 'dev')), may hold values from -8 to 8
- point_weight: float32 [128, 256], P(('grp', 'dev')), may hold values from 0.02 to 0.5
- exchange_kernel: float32 [128, 256], P(('grp', 'dev')), may hold values from -3 to -0.3
- atom_xyz: float32 [3, 1000], replicated, may hold values from -15 to 15
Outputs:
- response_hamiltonian: bfloat16 [64, 128, 128], P('dev')
- response_density: float32 [128, 256], P(('grp', 'dev'))
- multipoles: float32 [4, 1000], replicated
Inputs may be any that keep to these rules, and one draw needn't show every extreme that they name: `device_request`: row d belongs to device d of grp+dev in grp-major order. Each row has exactly 32 entries other than -1, distinct for one owner; in every group one owner is asked for 8 blocks by every device of the group. `batch_blocks`: every entry points to an entry of its device's request row that is not -1.
All inputs are finite; a program needn't handle non-finite values.
Results may differ from a plain program's by a relative error of at most 0.004.
Values may be sent and summed in bfloat16 or wider, within the bound.
A program may use at most 64 MiB of HBM per device.

v0:
```python
import jax
import jax.numpy as jnp
from jax import lax
from jax.sharding import PartitionSpec as P

HIGH = lax.Precision.HIGHEST


def far_field(multipoles, centre, offset, atom_xyz):
    gap = centre[:, None, None] + offset[:, :, None] - atom_xyz[:, None, :]
    inverse = lax.rsqrt(gap[0] * gap[0] + gap[1] * gap[1] + gap[2] * gap[2] + 1.0)
    cube = inverse * inverse * inverse
    dipole = multipoles[1] * gap[0] + multipoles[2] * gap[1] + multipoles[3] * gap[2]
    return jnp.sum(multipoles[0] * inverse + dipole * cube, axis=1)


def scaled_rows(values, factor):
    return (values.astype(jnp.float32) * factor[:, None]).astype(jnp.bfloat16)


def pair_terms(scaled, values, rel, tile):
    points = values.shape[0]
    return jnp.einsum(
        "rim,rjn->ijmn",
        scaled.reshape(-1, rel, tile),
        values.reshape(points, rel, tile),
        preferred_element_type=jnp.float32,
    )


def on_device(
    basis_values,
    stored_density_blocks,
    device_request,
    batch_blocks,
    batch_atom,
    point_offset,
    point_weight,
    exchange_kernel,
    atom_xyz,
):
    batches, points, width = basis_values.shape
    own, tile = (stored_density_blocks.shape[0], stored_density_blocks.shape[1])
    rel = width // tile
    wanted = device_request[0]
    owners, capacity = wanted.shape
    positions = owners * capacity
    atoms = atom_xyz.shape[1]
    picked = jnp.take(
        stored_density_blocks,
        jnp.clip(
            lax.all_to_all(wanted, "dev", split_axis=0, concat_axis=0, tiled=True), 0, own - 1
        ),
        axis=0,
    )
    fetched = lax.all_to_all(picked, "dev", split_axis=0, concat_axis=0, tiled=True)
    fetched = fetched.reshape(positions, tile, tile)

    def density_one(args):
        values, needed = args
        blocks = jnp.take(fetched, needed, axis=0).reshape(rel, rel, tile, tile)
        split = values.reshape(points, rel, tile)
        left = jnp.einsum("rim,ijmn->rijn", split, blocks, preferred_element_type=jnp.float32)
        return jnp.einsum("rijn,rjn->r", left, split.astype(jnp.float32))

    density_field = lax.map(density_one, (basis_values, batch_blocks))
    weighted = density_field * point_weight
    local_parts = jnp.stack(
        [
            jnp.sum(weighted, 1),
            jnp.sum(weighted * point_offset[0], 1),
            jnp.sum(weighted * point_offset[1], 1),
            jnp.sum(weighted * point_offset[2], 1),
        ]
    )
    onehot = (batch_atom[:, None] == jnp.arange(atoms, dtype=jnp.int32)[None, :]).astype(
        jnp.float32
    )
    local_moments = jnp.dot(local_parts, onehot, precision=HIGH)
    centres = jnp.dot(atom_xyz, onehot.T, precision=HIGH)
    xc_part = point_weight * exchange_kernel * density_field
    multipoles = lax.psum(local_moments, ("grp", "dev"))

    def potential_one(args):
        centre, offset = args
        return far_field(multipoles, centre, offset, atom_xyz)

    hartree_part = point_weight * lax.map(
        potential_one, (centres.T, jnp.moveaxis(point_offset, 1, 0))
    )

    def both_one(args):
        values, first, second = args
        stacked = jnp.concatenate([scaled_rows(values, first), scaled_rows(values, second)], axis=0)
        doubled = jnp.concatenate([values, values], axis=0)
        return pair_terms(stacked, doubled, rel, tile)

    terms = lax.map(both_one, (basis_values, xc_part, hartree_part))
    flat_terms = terms.reshape(batches * rel * rel, tile * tile)
    summed = jax.ops.segment_sum(flat_terms, batch_blocks.reshape(-1), num_segments=positions)
    outgoing = summed.astype(jnp.bfloat16).reshape(owners, capacity, tile, tile)
    received, received_ids = (
        lax.all_to_all(outgoing, "dev", split_axis=0, concat_axis=0, tiled=True),
        lax.all_to_all(wanted, "dev", split_axis=0, concat_axis=0, tiled=True),
    )
    owner_onehot = (
        jnp.arange(own, dtype=jnp.int32)[:, None] == received_ids.reshape(1, positions)
    ).astype(jnp.bfloat16)
    owned = jnp.dot(
        owner_onehot, received.reshape(positions, tile * tile), preferred_element_type=jnp.float32
    )
    total = lax.psum(owned, "grp")
    hamiltonian = total.astype(jnp.bfloat16).reshape(own, tile, tile)
    return (hamiltonian, density_field, multipoles)


def solution(mesh):
    return jax.shard_map(
        on_device,
        mesh=mesh,
        in_specs=(
            P(("grp", "dev"), None, None),
            P("dev", None, None),
            P(("grp", "dev"), None, None),
            P(("grp", "dev"), None),
            P(("grp", "dev")),
            P(None, ("grp", "dev"), None),
            P(("grp", "dev"), None),
            P(("grp", "dev"), None),
            P(),
        ),
        out_specs=(P("dev", None, None), P(("grp", "dev"), None), P()),
        check_vma=False,
    )
```

profile of v0, /device:TPU:0, one launch (start us, length us, event | category | flops | bytes accessed | tf_op | source)
XLA Modules:
  0.0 220.7 jit_solution(17259196471486747598)
XLA Ops:
  0.6 13.8 %all_to_all.20 = s32[8,1,8]{2,1,0:T(1,128)S(1)} all-to-all(s32[8,1,8]{2,1,0:T(1,128)} %bitcast.168), channel_id=1, replica_groups=mesh['grp'=4,'dev'=8] {'dev'}, dimensions={0} | all-to-all | bytes 512 | tf_op jit(solution)/shard_map/all_to_all | solution.py:104
  14.6 1.0 gather_fusion.1
  15.6 1.6 broadcast_select_fusion
  17.2 4.5 %all-to-all-start.1 = ((bf16[8,8,128,128]{3,2,1,0:T(8,128)(2,1)}), bf16[8,8,128,128]{3,2,1,0:T(8,128)(2,1)}, u32[]{:S(2)}, u32[]{:S(2)}) async-start(bf16[8,8,128,128]{3,2,1,0:T(8,128)(2,1)} %broadcast_select_fusion), calls=%async_computation.1 | async-start | bytes 4194304 | tf_op jit(solution)/shard_map/all_to_all | solution.py:56
  22.5 46.2 %all-to-all-done.1 = bf16[8,8,128,128]{3,2,1,0:T(8,128)(2,1)} async-done(((bf16[8,8,128,128]{3,2,1,0:T(8,128)(2,1)}), bf16[8,8,128,128]{3,2,1,0:T(8,128)(2,1)}, u32[]{:S(2)}, u32[]{:S(2)}) %all-to-all-start.1) | async-done | bytes 2097184 | tf_op jit(solution)/shard_map/all_to_all | solution.py:56
  68.8 12.6 %while.30 = (s32[]{:T(128)}, f32[4,256]{1,0:T(4,128)S(1)}, bf16[4,256,512]{1,2,0:T(8,128)(2,1)S(1)}, s32[4,16]{1,0:T(4,128)S(1)}, bf16[64,128,128]{2,1,0:T(8,128)(2,1)}, /*index=5*/s32[]{:T(128)}, s32[]{:T(128)}) while((s32[]{:T(128)}, f32[4,256]{1,0:T(4,128)S(1)}, bf16[4,256,512]{1,2,0:T(8,128)(2,1)S(1)}, s32[4,16]{1,0:T(4,128)S(1)}, ...), condition=%wide.region_1.2_spmd, body=%wide.region_0.1_spmd.sunk | while | flops 134874000 | bytes 2629349 | solution.py:66
  69.0 2.2 %gather_fusion = bf16[16,128,128]{2,1,0:T(8,128)(2,1)S(1)} fusion(bf16[64,128,128]{2,1,0:T(8,128)(2,1)} %get-tuple-element.346, s32[1024]{0:T(1024)S(1)} %pad_clamp_fusion.3), kind=kCustom, calls=%fused_computation.clone.1 | custom fusion | bytes 1048640 | tf_op jit(solution)/shard_map/while/body/eval_jaxpr/jit(_take)/gather | solution.py:61
  72.2 2.2 %gather_fusion = bf16[16,128,128]{2,1,0:T(8,128)(2,1)S(1)} fusion(bf16[64,128,128]{2,1,0:T(8,128)(2,1)} %get-tuple-element.346, s32[1024]{0:T(1024)S(1)} %pad_clamp_fusion.3), kind=kCustom, calls=%fused_computation.clone.1 | custom fusion | bytes 1048640 | tf_op jit(solution)/shard_map/while/body/eval_jaxpr/jit(_take)/gather | solution.py:61
  75.3 2.2 %gather_fusion = bf16[16,128,128]{2,1,0:T(8,128)(2,1)S(1)} fusion(bf16[64,128,128]{2,1,0:T(8,128)(2,1)} %get-tuple-element.346, s32[1024]{0:T(1024)S(1)} %pad_clamp_fusion.3), kind=kCustom, calls=%fused_computation.clone.1 | custom fusion | bytes 1048640 | tf_op jit(solution)/shard_map/while/body/eval_jaxpr/jit(_take)/gather | solution.py:61
  78.5 2.2 %gather_fusion = bf16[16,128,128]{2,1,0:T(8,128)(2,1)S(1)} fusion(bf16[64,128,128]{2,1,0:T(8,128)(2,1)} %get-tuple-element.346, s32[1024]{0:T(1024)S(1)} %pad_clamp_fusion.3), kind=kCustom, calls=%fused_computation.clone.1 | custom fusion | bytes 1048640 | tf_op jit(solution)/shard_map/while/body/eval_jaxpr/jit(_take)/gather | solution.py:61
  81.7 38.1 %psum.14 = f32[4,1000]{1,0:T(4,128)S(1)} all-reduce(f32[4,1000]{1,0:T(4,128)S(1)} %fusion.24), channel_id=1, replica_groups=mesh['grp'=4,'dev'=8] {'grp','dev'}, use_global_device_ids=true, to_apply=%region_6.7 | all-reduce | flops 4000 | bytes 32000 | tf_op jit(solution)/shard_map/psum | solution.py:82
  119.8 5.8 %while.31 = (s32[]{:T(128)}, f32[4,256]{1,0:T(4,128)S(1)}, f32[4,1000]{1,0:T(4,128)S(1)}, f32[4,3]{1,0:T(4,128)S(1)}, f32[4,3,256]{2,1,0:T(4,128)S(1)}, /*index=5*/f32[3,1000]{1,0:T(4,128)S(1)}, s32[]{:T(128)}, s32[]{:T(128)}) while((s32[]{:T(128)}, f32[4,256]{1,0:T(4,128)S(1)}, f32[4,1000]{1,0:T(4,128)S(1)}, f32[4,3]{1,0:T(4,128)S(1)}, ...), condition=%wide.region_9.10_spmd, body=%wide.region_7.9_spmd.sunk | while | flops 5120514 | bytes 6216429 | solution.py:88
  121.8 0.8 fusion.55
  123.3 0.8 fusion.55
  126.2 9.0 %while.32 = (s32[]{:T(128)}, f32[4,4,4,128,128]{4,3,2,1,0:T(8,128)}, bf16[4,256,512]{1,2,0:T(8,128)(2,1)S(1)}, f32[4,256]{1,0:T(4,128)S(1)}, f32[4,256]{1,0:T(4,128)S(1)}, /*index=5*/s32[]{:T(128)}) while((s32[]{:T(128)}, f32[4,4,4,128,128]{4,3,2,1,0:T(8,128)}, bf16[4,256,512]{1,2,0:T(8,128)(2,1)S(1)}, f32[4,256]{1,0:T(4,128)S(1)}, ...), condition=%wide.region_11.12_spmd, body=%wide.region_10.11_spmd.sunk | while | flops 271187968 | bytes 7870553 | solution.py:98
  127.4 1.1 constant_dynamic-update-slice_fusion.2
  129.6 1.1 constant_dynamic-update-slice_fusion.2
  131.9 1.1 constant_dynamic-update-slice_fusion.2
  134.2 1.1 constant_dynamic-update-slice_fusion.2
  135.2 11.4 %scatter_custom_fusion = f32[64,16384]{1,0:T(8,128)} fusion(s32[64]{0:T(128)S(1)} %reshape.178, f32[8,8,128,128]{3,2,1,0:T(8,128)} %bitcast.155, f32[]{:T(128)} %constant.70.clone.1), kind=kCustom, calls=%fused_computation.44 | custom fusion | flops 1048576 | bytes 8388612 | tf_op jit(solution)/shard_map/scatter-add | solution.py:100
  146.6 3.9 %convert_bitcast_fusion = bf16[8,8,128,128]{3,1,2,0:T(8,128)(2,1)} fusion(f32[64,16384]{1,0:T(8,128)} %scatter_custom_fusion), kind=kLoop, calls=%fused_computation.49 | loop fusion | flops 1048576 | bytes 6291456 | tf_op jit(solution)/shard_map/reshape | solution.py:101
  150.5 5.9 %all-to-all-start.2 = ((bf16[8,8,128,128]{3,1,2,0:T(8,128)(2,1)}), bf16[8,8,128,128]{3,1,2,0:T(8,128)(2,1)S(1)}, u32[]{:S(2)}, u32[]{:S(2)}) async-start(bf16[8,8,128,128]{3,1,2,0:T(8,128)(2,1)} %convert_bitcast_fusion), calls=%async_computation.2 | async-start | bytes 4194304 | tf_op jit(solution)/shard_map/all_to_all | solution.py:103
  157.7 45.4 %all-to-all-done.2 = bf16[8,8,128,128]{3,1,2,0:T(8,128)(2,1)S(1)} async-done(((bf16[8,8,128,128]{3,1,2,0:T(8,128)(2,1)}), bf16[8,8,128,128]{3,1,2,0:T(8,128)(2,1)S(1)}, u32[]{:S(2)}, u32[]{:S(2)}) %all-to-all-start.2) | async-done | bytes 2097184 | tf_op jit(solution)/shard_map/all_to_all | solution.py:103
  203.5 16.5 %all-reduce.1 = bf16[8,16384]{1,0:T(8,128)(2,1)S(1)} all-reduce(f32[8,16384]{1,0:T(8,128)S(1)} %fusion.20), channel_id=1, replica_groups=mesh['grp'=4,'dev'=8] {'grp'}, use_global_device_ids=true, to_apply=%region_13.14 | all-reduce | flops 131072 | bytes 786432 | tf_op jit(solution)/shard_map/psum | solution.py:112
  (122 shorter events, 16.4 us)
Async XLA Ops:
  0.6 14.0 %copy-start = (bf16[8,128,128]{2,1,0:T(8,128)(2,1)S(1)}, bf16[8,128,128]{2,1,0:T(8,128)(2,1)}, u32[]{:S(2)}) copy-start(bf16[8,128,128]{2,1,0:T(8,128)(2,1)} %param.16) | copy-start | bytes 786436
  15.6 6.1 %copy-start.8 = (s32[4,16]{1,0:T(4,128)S(1)}, s32[4,16]{1,0:T(4,128)}, u32[]{:S(2)}) copy-start(s32[4,16]{1,0:T(4,128)} %param.18) | copy-start | bytes 772
  15.6 6.2 %copy-start.4 = (f32[3,4,256]{2,1,0:T(4,128)S(1)}, f32[3,4,256]{2,1,0:T(4,128)}, u32[]{:S(2)}) copy-start(f32[3,4,256]{2,1,0:T(4,128)} %param.20) | copy-start | bytes 36868
  15.6 6.2 %copy-start.1 = (bf16[4,256,512]{2,1,0:T(8,128)(2,1)S(1)}, bf16[4,256,512]{2,1,0:T(8,128)(2,1)}, u32[]{:S(2)}) copy-start(bf16[4,256,512]{2,1,0:T(8,128)(2,1)} %param.15) | copy-start | bytes 3145732
  17.2 5.1 %copy-start.3 = (f32[3,1000]{1,0:T(4,128)S(1)}, f32[3,1000]{1,0:T(4,128)}, u32[]{:S(2)}) copy-start(f32[3,1000]{1,0:T(4,128)} %param.23) | copy-start | bytes 36004
  17.2 5.1 %copy-start.9 = (s32[4]{0:T(128)S(1)}, s32[4]{0:T(128)}, u32[]{:S(2)}) copy-start(s32[4]{0:T(128)} %param.19) | copy-start | bytes 52
  17.2 51.6 %all-to-all-start.1 = ((bf16[8,8,128,128]{3,2,1,0:T(8,128)(2,1)}), bf16[8,8,128,128]{3,2,1,0:T(8,128)(2,1)}, u32[]{:S(2)}, u32[]{:S(2)}) async-start(bf16[8,8,128,128]{3,2,1,0:T(8,128)(2,1)} %broadcast_select_fusion), calls=%async_computation.1 | async-start | bytes 4194304 | tf_op jit(solution)/shard_map/all_to_all | solution.py:56
  68.8 12.6 %copy-start.5 = (f32[4,256]{1,0:T(4,128)S(1)}, f32[4,256]{1,0:T(4,128)}, u32[]{:S(2)}) copy-start(f32[4,256]{1,0:T(4,128)} %param.21) | copy-start | bytes 12292
  68.8 12.6 %copy-start.7 = (f32[4,256]{1,0:T(4,128)S(1)}, f32[4,256]{1,0:T(4,128)}, u32[]{:S(2)}) copy-start(f32[4,256]{1,0:T(4,128)} %param.22) | copy-start | bytes 12292
  81.3 38.5 %copy-start.6 = (f32[4,256]{1,0:T(4,128)}, f32[4,256]{1,0:T(4,128)S(1)}, u32[]{:S(2)}) copy-start(f32[4,256]{1,0:T(4,128)S(1)} %get-tuple-element.165) | copy-start | bytes 12292
  125.6 0.6 copy-start.2
  150.5 52.6 %all-to-all-start.2 = ((bf16[8,8,128,128]{3,1,2,0:T(8,128)(2,1)}), bf16[8,8,128,128]{3,1,2,0:T(8,128)(2,1)S(1)}, u32[]{:S(2)}, u32[]{:S(2)}) async-start(bf16[8,8,128,128]{3,1,2,0:T(8,128)(2,1)} %convert_bitcast_fusion), calls=%async_computation.2 | async-start | bytes 4194304 | tf_op jit(solution)/shard_map/all_to_all | solution.py:103
where the time goes:
time: 221 us
  waiting for transfers between devices  91.6 us (41%)
  blocking collectives  68.4 us (31%)
  other arithmetic  24 us (11%)
  local copies, waits for them, and re-layouts  20.4 us (9%)
  starting transfers between devices  10.4 us (5%)
  matrix products  4.75 us (2%)
    all_to_all x1, waiting for transfers between devices, on_device(): lax.all_to_all(picked, 'dev', split_axis=0, concat_axis=0, tiled=True)  46.2 us
    all_to_all x1, waiting for transfers between devices, on_device(): lax.all_to_all(outgoing, 'dev', split_axis=0, concat_axis=0, tiled=True)  45.4 us
    psum x1, blocking collectives, on_device(): multipoles = lax.psum(local_moments, ('grp', 'dev'))  38.1 us
    psum x1, blocking collectives, on_device(): total = lax.psum(owned, 'grp')  16.5 us
    all_to_all x1, blocking collectives, on_device(): lax.all_to_all(wanted, 'dev', split_axis=0, concat_axis=0, tiled=True)  13.8 us
    scatter-add x1, other arithmetic, on_device(): jax.ops.segment_sum(flat_terms, batch_blocks.reshape(-1), num_segments=po...  11.4 us
    gather x4, local copies, waits for them, and re-layouts, density_one(): blocks = jnp.take(fetched, needed, axis=0).reshape(rel, rel, tile, tile)  8.95 us
    all_to_all x1, starting transfers between devices, on_device(): lax.all_to_all(outgoing, 'dev', split_axis=0, concat_axis=0, tiled=True)  5.93 us
  transfers between devices with their start and end apart: 2, of which 2 were waited for; matrix products, arithmetic and copies ran while one was open for 1% of the time, Pallas kernels for 0%

commit v1 on v0

v1 whole, which is shorter than its diff:
```python
import functools

import jax
import jax.numpy as jnp
from jax import lax
from jax.experimental import pallas as pl
from jax.experimental.pallas import tpu as pltpu
from jax.sharding import PartitionSpec as P

MESH = pl.DeviceIdType.MESH
LANES = 128
VMEM = pl.BlockSpec(memory_space=pltpu.VMEM)
SMEM = pl.BlockSpec(memory_space=pltpu.SMEM)
ANY = pl.BlockSpec(memory_space=pl.ANY)
F32 = jnp.float32
BF16 = jnp.bfloat16


def remote(src, dst, send, recv, grp, dev):
    return pltpu.make_async_remote_copy(
        src_ref=src,
        dst_ref=dst,
        send_sem=send,
        recv_sem=recv,
        device_id=(grp, dev),
        device_id_type=MESH,
    )


def meet(peers):
    barrier = pltpu.get_barrier_semaphore()
    for grp, dev in peers:
        pl.semaphore_signal(barrier, inc=1, device_id=(grp, dev), device_id_type=MESH)
    pl.semaphore_wait(barrier, len(peers))


def slot_of(request, blocks, b, p, capacity, own):
    position = blocks[b, p]
    return (position // capacity) * own + request[position]


def density_kernel(
    groups,
    devs,
    capacity,
    stored,
    request,
    blocks,
    batch_atom,
    offset,
    weight,
    xyz,
    values_any,
    density,
    own_rows,
    table_out,
    values,
    gathered,
    table,
    local_sem,
    send_a,
    recv_a,
    send_b,
    recv_b,
    send_c,
    recv_c,
    send_d,
    recv_d,
):
    g, me = lax.axis_index("grp"), lax.axis_index("dev")
    own, tile = stored.shape[0], stored.shape[1]
    batches, points, width = values.shape
    rel = width // tile
    atoms = xyz.shape[1]
    half = own // 2
    core = lax.rem(g, 2)
    pair = g + 1 - 2 * core

    load = pltpu.make_async_copy(values_any, values, local_sem.at[0])
    load.start()
    mine = pltpu.make_async_copy(
        stored, gathered.at[pl.ds(me * own, own)], local_sem.at[1]
    )
    mine.start()
    peers = [(g, lax.rem(me + k, devs)) for k in range(1, devs)]
    peers += [(lax.rem(g + j, groups), me) for j in range(1, groups)]
    meet(peers)

    out = []
    for k in range(1, devs):
        copy = remote(
            stored.at[pl.ds(core * half, half)],
            gathered.at[pl.ds(me * own + core * half, half)],
            send_a.at[k],
            recv_a.at[k],
            g,
            lax.rem(me + k, devs),
        )
        copy.start()
        out.append(copy)

    centres = []
    spot = lax.broadcasted_iota(jnp.int32, (3, atoms), 1)
    for b in range(batches):
        centres.append(
            jnp.sum(jnp.where(spot == batch_atom[b], xyz[...], 0.0), axis=1, keepdims=True)
        )

    passed = []
    for k in range(1, devs):
        out[k - 1].wait_recv()
        rows = pl.ds(lax.rem(me + devs - k, devs) * own + core * half, half)
        copy = remote(
            gathered.at[rows], gathered.at[rows], send_b.at[k], recv_b.at[k], pair, me
        )
        copy.start()
        passed.append(copy)
    load.wait()
    mine.wait()
    for copy in passed:
        copy.wait_recv()

    lane = lax.broadcasted_iota(jnp.int32, (1, LANES), 1)
    for b in range(batches):
        matrix = jnp.concatenate(
            [
                jnp.concatenate(
                    [
                        gathered[slot_of(request, blocks, b, i * rel + j, capacity, own)]
                        for j in range(rel)
                    ],
                    axis=1,
                )
                for i in range(rel)
            ],
            axis=0,
        )
        left = jnp.dot(values[b], matrix, preferred_element_type=F32)
        product = left * values[b].astype(F32)
        folded = product[:, :tile]
        for i in range(1, rel):
            folded = folded + product[:, i * tile : (i + 1) * tile]
        row = jnp.sum(folded.T, axis=0, keepdims=True)
        density[pl.ds(b, 1), :] = row
        weighted = row * weight[pl.ds(b, 1), :]
        parts = [jnp.sum(weighted, axis=1, keepdims=True)]
        for k in range(3):
            parts.append(
                jnp.sum(weighted * offset[k, pl.ds(b, 1), :], axis=1, keepdims=True)
            )
        parts += [centres[b][k : k + 1] for k in range(3)]
        entry = jnp.zeros((1, LANES), F32) + batch_atom[b].astype(F32)
        for k, part in enumerate(parts):
            entry = jnp.where(lane == k, part, entry)
        own_rows[pl.ds(b, 1), :] = entry
        table[me, g, pl.ds(b, 1), :] = entry

    first = []
    for j in range(1, groups):
        copy = remote(
            table.at[me, g],
            table.at[me, g],
            send_c.at[j],
            recv_c.at[j],
            lax.rem(g + j, groups),
            me,
        )
        copy.start()
        first.append(copy)
    for copy in first:
        copy.wait_recv()
    second = []
    for k in range(1, devs):
        copy = remote(
            table.at[me], table.at[me], send_d.at[k], recv_d.at[k], g, lax.rem(me + k, devs)
        )
        copy.start()
        second.append(copy)
    for copy in out + passed + first:
        copy.wait_send()
    for copy in second:
        copy.wait_recv()
    for copy in second:
        copy.wait_send()
    for d in range(devs):
        table_out[d * groups : (d + 1) * groups] = table[d]


def term_kernel(
    capacity,
    own,
    request,
    blocks,
    values,
    table,
    own_rows,
    density,
    weight,
    exchange,
    offset,
    part,
    multipoles,
    total,
):
    batches, points, width = values.shape
    tile = part.shape[1]
    rel = width // tile
    devices = table.shape[0]
    atoms = multipoles.shape[1]
    chunk = min(devices, 32)
    total[...] = jnp.zeros_like(total)

    places = [
        [own_rows[pl.ds(b, 1), 4 + k : 5 + k] + offset[k, pl.ds(b, 1), :] for k in range(3)]
        for b in range(batches)
    ]
    spot = lax.broadcasted_iota(jnp.int32, (1, atoms), 1).astype(F32)

    def gather(step, carry):
        fields, moments = carry
        fields, moments = list(fields), list(moments)
        for source in range(batches):
            rows = table[pl.ds(step * chunk, chunk), source, :]
            column = [rows[:, k : k + 1] for k in range(8)]
            hit = column[7] == spot
            for k in range(4):
                moments[k] = moments[k] + jnp.sum(
                    jnp.where(hit, column[k], 0.0), axis=0, keepdims=True
                )
            for b in range(batches):
                gap = [places[b][k] - column[4 + k] for k in range(3)]
                inverse = lax.rsqrt(
                    gap[0] * gap[0] + gap[1] * gap[1] + gap[2] * gap[2] + 1.0
                )
                cube = inverse * inverse * inverse
                dipole = column[1] * gap[0] + column[2] * gap[1] + column[3] * gap[2]
                fields[b] = fields[b] + jnp.sum(
                    column[0] * inverse + dipole * cube, axis=0, keepdims=True
                )
        return tuple(fields), tuple(moments)

    carry = (
        tuple(jnp.zeros((1, points), F32) for _ in range(batches)),
        tuple(jnp.zeros((1, atoms), F32) for _ in range(4)),
    )
    if devices == chunk:
        fields, moments = gather(0, carry)
    else:
        fields, moments = lax.fori_loop(0, devices // chunk, gather, carry)
    for k in range(4):
        multipoles[pl.ds(k, 1), :] = moments[k]

    for b in range(batches):
        pick = pl.ds(b, 1)
        factors = (
            weight[pick, :] * exchange[pick, :] * density[pick, :],
            weight[pick, :] * fields[b],
        )
        wide = values[b].astype(F32)
        scaled = []
        for factor in factors:
            column = jnp.broadcast_to(factor, (tile, points)).T
            scaled.append(
                jnp.concatenate(
                    [
                        (wide[:, i * tile : (i + 1) * tile] * column).astype(BF16)
                        for i in range(rel)
                    ],
                    axis=1,
                )
            )
        stacked = jnp.concatenate(scaled, axis=0)
        doubled = jnp.concatenate([values[b], values[b]], axis=0)
        term = lax.dot_general(
            stacked, doubled, (((0,), (0,)), ((), ())), preferred_element_type=F32
        )
        for i in range(rel):
            for j in range(rel):
                slot = slot_of(request, blocks, b, i * rel + j, capacity, own)
                total[slot] += term[i * tile : (i + 1) * tile, j * tile : (j + 1) * tile]
    part[...] = total[...].astype(BF16)


def reduce_kernel(
    groups,
    devs,
    part,
    result,
    paired,
    outgoing,
    arrived,
    across,
    final,
    send_a,
    recv_a,
    send_b,
    recv_b,
    send_c,
    recv_c,
    send_d,
    recv_d,
):
    g, me = lax.axis_index("grp"), lax.axis_index("dev")
    own = result.shape[0]
    half = own // 2
    lines = groups // 2
    core = lax.rem(g, 2)
    line = g // 2
    pair = g + 1 - 2 * core

    peers = [(pair, me)]
    peers += [(g, lax.rem(me + k, devs)) for k in range(1, devs)]
    peers += [(lax.rem(line + j, lines) * 2 + core, me) for j in range(1, lines)]
    meet(peers)

    order = list(range(1, devs)) + [0]
    halves = {}
    for k in order:
        owner = lax.rem(me + k, devs)
        copy = remote(
            part.at[pl.ds(owner * own + (1 - core) * half, half)],
            paired.at[k],
            send_a.at[k],
            recv_a.at[k],
            pair,
            me,
        )
        copy.start()
        halves[k] = copy

    def sum_of_pair(k):
        owner = lax.rem(me + k, devs)
        here = part[pl.ds(owner * own + core * half, half)]
        return here.astype(F32) + paired[k].astype(F32)

    out = []
    for k in range(1, devs):
        halves[k].wait_recv()
        outgoing[k] = sum_of_pair(k).astype(BF16)
        copy = remote(
            outgoing.at[k],
            arrived.at[k],
            send_b.at[k],
            recv_b.at[k],
            g,
            lax.rem(me + k, devs),
        )
        copy.start()
        out.append(copy)
    halves[0].wait_recv()
    summed = sum_of_pair(0)
    for k in range(1, devs):
        out[k - 1].wait_recv()
        summed = summed + arrived[k].astype(F32)
    across[line] = summed.astype(BF16)
    rows = []
    for j in range(1, lines):
        copy = remote(
            across.at[line],
            across.at[line],
            send_c.at[j],
            recv_c.at[j],
            lax.rem(line + j, lines) * 2 + core,
            me,
        )
        copy.start()
        rows.append(copy)
    for copy in rows:
        copy.wait_recv()
    whole = across[0].astype(F32)
    for j in range(1, lines):
        whole = whole + across[j].astype(F32)
    final[pl.ds(core * half, half)] = whole.astype(BF16)
    last = remote(
        final.at[pl.ds(core * half, half)],
        final.at[pl.ds(core * half, half)],
        send_d,
        recv_d,
        pair,
        me,
    )
    last.start()
    for copy in list(halves.values()) + out + rows:
        copy.wait_send()
    last.wait_recv()
    last.wait_send()
    result[...] = final[...]


def on_device(
    groups,
    devs,
    basis_values,
    stored_density_blocks,
    device_request,
    batch_blocks,
    batch_atom,
    point_offset,
    point_weight,
    exchange_kernel,
    atom_xyz,
):
    batches, points, width = basis_values.shape
    own, tile = stored_density_blocks.shape[:2]
    owners, capacity = device_request.shape[1:]
    slots = devs * own
    atoms = atom_xyz.shape[1]
    half = own // 2
    request = device_request.reshape(owners * capacity)
    dma = pltpu.SemaphoreType.DMA

    density, own_rows, table = pl.pallas_call(
        functools.partial(density_kernel, groups, devs, capacity),
        out_shape=(
            jax.ShapeDtypeStruct((batches, points), F32),
            jax.ShapeDtypeStruct((batches, LANES), F32),
            jax.ShapeDtypeStruct((devs * groups, batches, LANES), F32),
        ),
        in_specs=[VMEM, SMEM, SMEM, SMEM, VMEM, VMEM, VMEM, ANY],
        out_specs=(VMEM, VMEM, VMEM),
        scratch_shapes=[
            pltpu.VMEM((batches, points, width), BF16),
            pltpu.VMEM((slots, tile, tile), BF16),
            pltpu.VMEM((devs, groups, batches, LANES), F32),
            dma((2,)),
            dma((devs,)),
            dma((devs,)),
            dma((devs,)),
            dma((devs,)),
            dma((groups,)),
            dma((groups,)),
            dma((devs,)),
            dma((devs,)),
        ],
        compiler_params=pltpu.CompilerParams(collective_id=0, has_side_effects=True),
    )(
        stored_density_blocks,
        request,
        batch_blocks,
        batch_atom,
        point_offset,
        point_weight,
        atom_xyz,
        basis_values,
    )

    part, multipoles = pl.pallas_call(
        functools.partial(term_kernel, capacity, own),
        out_shape=(
            jax.ShapeDtypeStruct((slots, tile, tile), BF16),
            jax.ShapeDtypeStruct((4, atoms), F32),
        ),
        in_specs=[SMEM, SMEM, VMEM, VMEM, VMEM, VMEM, VMEM, VMEM, VMEM],
        out_specs=(VMEM, VMEM),
        scratch_shapes=[pltpu.VMEM((slots, tile, tile), F32)],
    )(
        request,
        batch_blocks,
        basis_values,
        table,
        own_rows,
        density,
        point_weight,
        exchange_kernel,
        point_offset,
    )

    hamiltonian = pl.pallas_call(
        functools.partial(reduce_kernel, groups, devs),
        out_shape=jax.ShapeDtypeStruct((own, tile, tile), BF16),
        in_specs=[VMEM],
        out_specs=VMEM,
        scratch_shapes=[
            pltpu.VMEM((devs, half, tile, tile), BF16),
            pltpu.VMEM((devs, half, tile, tile), BF16),
            pltpu.VMEM((devs, half, tile, tile), BF16),
            pltpu.VMEM((groups // 2, half, tile, tile), BF16),
            pltpu.VMEM((own, tile, tile), BF16),
            dma((devs,)),
            dma((devs,)),
            dma((devs,)),
            dma((devs,)),
            dma((groups // 2,)),
            dma((groups // 2,)),
            dma,
            dma,
        ],
        compiler_params=pltpu.CompilerParams(collective_id=1, has_side_effects=True),
    )(part)
    return (hamiltonian, density, multipoles)


def solution(mesh):
    return jax.shard_map(
        functools.partial(on_device, mesh.shape["grp"], mesh.shape["dev"]),
        mesh=mesh,
        in_specs=(
            P(("grp", "dev"), None, None),
            P("dev", None, None),
            P(("grp", "dev"), None, None),
            P(("grp", "dev"), None),
            P(("grp", "dev")),
            P(None, ("grp", "dev"), None),
            P(("grp", "dev"), None),
            P(("grp", "dev"), None),
            P(),
        ),
        out_specs=(P("dev", None, None), P(("grp", "dev"), None), P()),
        check_vma=False,
    )
```

time: 221 us -> 85.7 us (0.39)
  the two profiles are of different devices: /device:TPU:0 before, /device:TPU:15 now
where the time goes in v1:
time: 85.7 us; the launch traced here: 85.5 us
  Pallas kernels  81.3 us (95%)
  local copies, waits for them, and re-layouts  3.55 us (4%)
    pallas_call x1, Pallas kernels, on_device(): pl.pallas_call(functools.partial(reduce_kernel, groups, devs), out_shape=...  38.2 us
    pallas_call x1, Pallas kernels, on_device(): pl.pallas_call(functools.partial(density_kernel, groups, devs, capacity),...  36.9 us
    pallas_call x1, Pallas kernels, on_device(): pl.pallas_call(functools.partial(term_kernel, capacity, own), out_shape=(...  6.18 us
    unnamed x4, local copies, waits for them, and re-layouts  2.27 us

profile of v1, /device:TPU:15, one launch (start us, length us, event | category | flops | bytes accessed | tf_op | source)
XLA Modules:
  0.0 85.5 jit_solution(10544402018794168482)
XLA Ops:
  0.6 1.3 %reshape.9.request = s32[64]{0:T(128)} reshape(s32[1,8,8]{2,1,0:T(8,128)} %param.11) | data formatting | bytes 512 | tf_op jit(solution)/shard_map/reshape | solution.py:409
  1.9 36.9 %shard_map.112 = (f32[4,256]{1,0:T(4,128)}, f32[4,128]{1,0:T(4,128)}, f32[32,4,128]{2,1,0:T(4,128)}) custom-call(bf16[8,128,128]{2,1,0:T(8,128)(2,1)} %stored.1, s32[64]{0:T(128)} %reshape.9.request, s32[4,16]{1,0:T(4,128)} %blocks.3, s32[4]{0:T(128)} %batch_atom.1, f32[3,4,256]{2,1,0:T(4,128)} %offset.3, f32[4,256]{1,0:T(4,128)} %weight.3, f32[3,1000]{1,0:T(4,128)} %xyz.1, ...), custom_call_target="tpu_custom_call" | custom-call | tf_op jit(solution)/shard_map/pallas_call | solution.py:412
  38.8 0.0 copy-start
  38.9 6.2 %shard_map.113 = (bf16[64,128,128]{2,1,0:T(8,128)(2,1)}, f32[4,1000]{1,0:T(4,128)}) custom-call(s32[64]{0:T(128)} %reshape.9.request, s32[4,16]{1,0:T(4,128)} %blocks.3, bf16[4,256,512]{2,1,0:T(8,128)(2,1)} %values.1, f32[32,4,128]{2,1,0:T(4,128)} %get-tuple-element.8.table, f32[4,128]{1,0:T(4,128)} %get-tuple-element.9.own_rows, ...), custom_call_target="tpu_custom_call" | custom-call | tf_op jit(solution)/shard_map/pallas_call | solution.py:447
  45.0 38.2 %shard_map.114 = bf16[8,128,128]{2,1,0:T(8,128)(2,1)} custom-call(bf16[64,128,128]{2,1,0:T(8,128)(2,1)} %get-tuple-element.11.part), custom_call_target="tpu_custom_call" | custom-call | tf_op jit(solution)/shard_map/pallas_call | solution.py:468
  83.2 1.7 %copy.14 = bf16[8,128,128]{2,1,0:T(8,128)(2,1)} copy(bf16[8,128,128]{2,1,0:T(8,128)(2,1)} %shard_map.114) | data formatting | bytes 524288
  84.9 0.0 copy-done
  84.9 0.6 copy.15
Async XLA Ops:
  38.8 46.1 %copy-start = (f32[4,256]{1,0:T(4,128)S(1)}, f32[4,256]{1,0:T(4,128)}, u32[]{:S(2)}) copy-start(f32[4,256]{1,0:T(4,128)} %get-tuple-element.17.density) | copy-start | bytes 12292

commit v2 on v1

--- a/solution.py
+++ b/solution.py
@@ -36,7 +36,18 @@
 
 def slot_of(request, blocks, b, p, capacity, own):
     position = blocks[b, p]
-    return (position // capacity) * own + request[position]
+    owner = position // capacity
+    return owner * own + request[0, owner, position - owner * capacity]
+
+
+def flip(index, mask):
+    out = index
+    bit = 1
+    while bit <= mask:
+        if mask & bit:
+            out = out + bit - 2 * bit * lax.rem(index // bit, 2)
+        bit *= 2
+    return out
 
 
 def density_kernel(
@@ -60,6 +71,8 @@
     local_sem,
     send_a,
     recv_a,
+    send_y,
+    recv_y,
     send_b,
     recv_b,
     send_c,
@@ -72,9 +85,9 @@
     batches, points, width = values.shape
     rel = width // tile
     atoms = xyz.shape[1]
-    half = own // 2
-    core = lax.rem(g, 2)
-    pair = g + 1 - 2 * core
+    half, quarter = own // 2, own // 4
+    first_row = lax.rem(g, 2) * half
+    lane_row = first_row + lax.rem(g // 2, 2) * quarter
 
     load = pltpu.make_async_copy(values_any, values, local_sem.at[0])
     load.start()
@@ -86,18 +99,31 @@
     peers += [(lax.rem(g + j, groups), me) for j in range(1, groups)]
     meet(peers)
 
-    out = []
-    for k in range(1, devs):
-        copy = remote(
-            stored.at[pl.ds(core * half, half)],
-            gathered.at[pl.ds(me * own + core * half, half)],
-            send_a.at[k],
-            recv_a.at[k],
+    def piece(k):
+        return pl.ds(flip(me, k) * own + lane_row, quarter)
+
+    def source(k):
+        return stored.at[pl.ds(lane_row, quarter)] if k == 0 else gathered.at[piece(k)]
+
+    came = {}
+
+    def onward(k):
+        came[k + 1] = remote(
+            source(k),
+            gathered.at[piece(k)],
+            send_a.at[k + 1],
+            recv_a.at[k + 1],
             g,
-            lax.rem(me + k, devs),
-        )
-        copy.start()
-        out.append(copy)
+            flip(me, 1),
+        )
+        came[k + 1].start()
+
+    onward(0)
+    for k in range(2, devs, 2):
+        came[k] = remote(
+            source(0), gathered.at[piece(0)], send_a.at[k], recv_a.at[k], g, flip(me, k)
+        )
+        came[k].start()
 
     centres = []
     spot = lax.broadcasted_iota(jnp.int32, (3, atoms), 1)
@@ -106,15 +132,39 @@
             jnp.sum(jnp.where(spot == batch_atom[b], xyz[...], 0.0), axis=1, keepdims=True)
         )
 
-    passed = []
-    for k in range(1, devs):
-        out[k - 1].wait_recv()
-        rows = pl.ds(lax.rem(me + devs - k, devs) * own + core * half, half)
+    order = []
+    for k in range(2, devs, 2):
+        order += [k, k - 1]
+    order.append(devs - 1)
+    sideways, passed = {}, []
+
+    def hand_over(k):
+        sideways[k].wait_recv()
+        rows = pl.ds(flip(me, k) * own + first_row, half)
         copy = remote(
-            gathered.at[rows], gathered.at[rows], send_b.at[k], recv_b.at[k], pair, me
+            gathered.at[rows], gathered.at[rows], send_b.at[k], recv_b.at[k], flip(g, 1), me
         )
         copy.start()
         passed.append(copy)
+
+    for step, k in enumerate(order):
+        came[k].wait_recv()
+        sideways[k] = remote(
+            gathered.at[piece(k)],
+            gathered.at[piece(k)],
+            send_y.at[k],
+            recv_y.at[k],
+            flip(g, 2),
+            me,
+        )
+        sideways[k].start()
+        if k % 2 == 0:
+            onward(k)
+        if step >= 2:
+            hand_over(order[step - 2])
+    for k in order[-2:]:
+        hand_over(k)
+    out = list(came.values()) + list(sideways.values())
     load.wait()
     mine.wait()
     for copy in passed:
@@ -200,6 +250,7 @@
     offset,
     part,
     multipoles,
+    density_out,
     total,
 ):
     batches, points, width = values.shape
@@ -209,6 +260,7 @@
     atoms = multipoles.shape[1]
     chunk = min(devices, 32)
     total[...] = jnp.zeros_like(total)
+    density_out[...] = density[...]
 
     places = [
         [own_rows[pl.ds(b, 1), 4 + k : 5 + k] + offset[k, pl.ds(b, 1), :] for k in range(3)]
@@ -287,12 +339,16 @@
     part,
     result,
     paired,
+    sent_y,
+    came_y,
     outgoing,
     arrived,
     across,
     final,
     send_a,
     recv_a,
+    send_y,
+    recv_y,
     send_b,
     recv_b,
     send_c,
@@ -302,88 +358,91 @@
 ):
     g, me = lax.axis_index("grp"), lax.axis_index("dev")
     own = result.shape[0]
-    half = own // 2
-    lines = groups // 2
-    core = lax.rem(g, 2)
-    line = g // 2
-    pair = g + 1 - 2 * core
-
-    peers = [(pair, me)]
-    peers += [(g, lax.rem(me + k, devs)) for k in range(1, devs)]
-    peers += [(lax.rem(line + j, lines) * 2 + core, me) for j in range(1, lines)]
+    half, quarter = own // 2, own // 4
+    quads = groups // 4
+    quad, lane = g // 4, lax.rem(g, 4)
+    core, side = lax.rem(g, 2), lax.rem(g // 2, 2)
+    pair, beside = flip(g, 1), flip(g, 2)
+
+    peers = [(pair, me), (beside, me)]
+    peers += [(g, flip(me, k)) for k in range(1, devs)]
+    peers += [(lax.rem(quad + j, quads) * 4 + lane, me) for j in range(1, quads)]
     meet(peers)
 
-    order = list(range(1, devs)) + [0]
-    halves = {}
+    order = list(range(devs - 1, -1, -1))
+    halves, rows, out = {}, {}, {}
     for k in order:
-        owner = lax.rem(me + k, devs)
-        copy = remote(
-            part.at[pl.ds(owner * own + (1 - core) * half, half)],
+        halves[k] = remote(
+            part.at[pl.ds(flip(me, k) * own + (1 - core) * half, half)],
             paired.at[k],
             send_a.at[k],
             recv_a.at[k],
             pair,
             me,
         )
+        halves[k].start()
+
+    def sum_of_pair(k, which):
+        here = part[pl.ds(flip(me, k) * own + core * half + which * quarter, quarter)]
+        there = paired[k, pl.ds(which * quarter, quarter)]
+        return here.astype(F32) + there.astype(F32)
+
+    def sum_of_four(k):
+        rows[k].wait_recv()
+        return sum_of_pair(k, side) + came_y[k].astype(F32)
+
+    def to_owner(k):
+        outgoing[k] = sum_of_four(k).astype(BF16)
+        out[k] = remote(
+            outgoing.at[k], arrived.at[k], send_b.at[k], recv_b.at[k], g, flip(me, k)
+        )
+        out[k].start()
+
+    for step, k in enumerate(order):
+        halves[k].wait_recv()
+        sent_y[k] = sum_of_pair(k, 1 - side).astype(BF16)
+        rows[k] = remote(
+            sent_y.at[k], came_y.at[k], send_y.at[k], recv_y.at[k], beside, me
+        )
+        rows[k].start()
+        if step >= 2:
+            to_owner(order[step - 2])
+    to_owner(1)
+    whole = sum_of_four(0)
+    for k in order[:-1]:
+        out[k].wait_recv()
+        whole = whole + arrived[k].astype(F32)
+    others = []
+    if quads > 1:
+        across[quad] = whole.astype(BF16)
+        for j in range(1, quads):
+            copy = remote(
+                across.at[quad],
+                across.at[quad],
+                send_c.at[j],
+                recv_c.at[j],
+                lax.rem(quad + j, quads) * 4 + lane,
+                me,
+            )
+            copy.start()
+            others.append(copy)
+        for copy in others:
+            copy.wait_recv()
+        whole = across[0].astype(F32)
+        for j in range(1, quads):
+            whole = whole + across[j].astype(F32)
+    part_rows = pl.ds(core * half + side * quarter, quarter)
+    half_rows = pl.ds(core * half, half)
+    final[part_rows] = whole.astype(BF16)
+    for step, (where, to) in enumerate(((part_rows, beside), (half_rows, pair))):
+        copy = remote(
+            final.at[where], final.at[where], send_d.at[step], recv_d.at[step], to, me
+        )
         copy.start()
-        halves[k] = copy
-
-    def sum_of_pair(k):
-        owner = lax.rem(me + k, devs)
-        here = part[pl.ds(owner * own + core * half, half)]
-        return here.astype(F32) + paired[k].astype(F32)
-
-    out = []
-    for k in range(1, devs):
-        halves[k].wait_recv()
-        outgoing[k] = sum_of_pair(k).astype(BF16)
-        copy = remote(
-            outgoing.at[k],
-            arrived.at[k],
-            send_b.at[k],
-            recv_b.at[k],
-            g,
-            lax.rem(me + k, devs),
-        )
-        copy.start()
-        out.append(copy)
-    halves[0].wait_recv()
-    summed = sum_of_pair(0)
-    for k in range(1, devs):
-        out[k - 1].wait_recv()
-        summed = summed + arrived[k].astype(F32)
-    across[line] = summed.astype(BF16)
-    rows = []
-    for j in range(1, lines):
-        copy = remote(
-            across.at[line],
-            across.at[line],
-            send_c.at[j],
-            recv_c.at[j],
-            lax.rem(line + j, lines) * 2 + core,
-            me,
-        )
-        copy.start()
-        rows.append(copy)
-    for copy in rows:
         copy.wait_recv()
-    whole = across[0].astype(F32)
-    for j in range(1, lines):
-        whole = whole + across[j].astype(F32)
-    final[pl.ds(core * half, half)] = whole.astype(BF16)
-    last = remote(
-        final.at[pl.ds(core * half, half)],
-        final.at[pl.ds(core * half, half)],
-        send_d,
-        recv_d,
-        pair,
-        me,
-    )
-    last.start()
-    for copy in list(halves.values()) + out + rows:
+        others.append(copy)
+    for copy in [*halves.values(), *rows.values(), *out.values(), *others]:
         copy.wait_send()
-    last.wait_recv()
-    last.wait_send()
     result[...] = final[...]
 
 
@@ -402,11 +461,11 @@
 ):
     batches, points, width = basis_values.shape
     own, tile = stored_density_blocks.shape[:2]
-    owners, capacity = device_request.shape[1:]
+    capacity = device_request.shape[2]
     slots = devs * own
     atoms = atom_xyz.shape[1]
-    half = own // 2
-    request = device_request.reshape(owners * capacity)
+    half, quarter = own // 2, own // 4
+    request = device_request
     dma = pltpu.SemaphoreType.DMA
 
     density, own_rows, table = pl.pallas_call(
@@ -427,6 +486,8 @@
             dma((devs,)),
             dma((devs,)),
             dma((devs,)),
+            dma((devs,)),
+            dma((devs,)),
             dma((groups,)),
             dma((groups,)),
             dma((devs,)),
@@ -444,14 +505,15 @@
         basis_values,
     )
 
-    part, multipoles = pl.pallas_call(
+    part, multipoles, density = pl.pallas_call(
         functools.partial(term_kernel, capacity, own),
         out_shape=(
             jax.ShapeDtypeStruct((slots, tile, tile), BF16),
             jax.ShapeDtypeStruct((4, atoms), F32),
+            jax.ShapeDtypeStruct((batches, points), F32),
         ),
         in_specs=[SMEM, SMEM, VMEM, VMEM, VMEM, VMEM, VMEM, VMEM, VMEM],
-        out_specs=(VMEM, VMEM),
+        out_specs=(VMEM, VMEM, VMEM),
         scratch_shapes=[pltpu.VMEM((slots, tile, tile), F32)],
     )(
         request,
@@ -472,18 +534,22 @@
         out_specs=VMEM,
         scratch_shapes=[
             pltpu.VMEM((devs, half, tile, tile), BF16),
-            pltpu.VMEM((devs, half, tile, tile), BF16),
-            pltpu.VMEM((devs, half, tile, tile), BF16),
-            pltpu.VMEM((groups // 2, half, tile, tile), BF16),
+            pltpu.VMEM((devs, quarter, tile, tile), BF16),
+            pltpu.VMEM((devs, quarter, tile, tile), BF16),
+            pltpu.VMEM((devs, quarter, tile, tile), BF16),
+            pltpu.VMEM((devs, quarter, tile, tile), BF16),
+            pltpu.VMEM((groups // 4, quarter, tile, tile), BF16),
             pltpu.VMEM((own, tile, tile), BF16),
             dma((devs,)),
             dma((devs,)),
             dma((devs,)),
             dma((devs,)),
-            dma((groups // 2,)),
-            dma((groups // 2,)),
-            dma,
-            dma,
+            dma((devs,)),
+            dma((devs,)),
+            dma((groups // 4,)),
+            dma((groups // 4,)),
+            dma((2,)),
+            dma((2,)),
         ],
         compiler_params=pltpu.CompilerParams(collective_id=1, has_side_effects=True),
     )(part)

time: 85.7 us -> 68.3 us (0.80)
  the two profiles are of different devices: /device:TPU:15 before, /device:TPU:0 now
where the time goes in v2:
time: 68.3 us; the launch traced here: 68.1 us
  Pallas kernels  65.8 us (96%)
  local copies, waits for them, and re-layouts  1.67 us (2%)
    pallas_call x1, Pallas kernels, on_device(): pl.pallas_call(functools.partial(density_kernel, groups, devs, capacity),...  31.9 us
    pallas_call x1, Pallas kernels, on_device(): pl.pallas_call(functools.partial(reduce_kernel, groups, devs), out_shape=...  27.6 us
    pallas_call x1, Pallas kernels, on_device(): pl.pallas_call(functools.partial(term_kernel, capacity, own), out_shape=(...  6.24 us
    unnamed x1, local copies, waits for them, and re-layouts  1.67 us

profile of v2, /device:TPU:0, one launch (start us, length us, event | category | flops | bytes accessed | tf_op | source)
XLA Modules:
  0.0 68.1 jit_solution(8257860943447381525)
XLA Ops:
  0.6 31.9 %shard_map.112 = (f32[4,256]{1,0:T(4,128)}, f32[4,128]{1,0:T(4,128)}, f32[32,4,128]{2,1,0:T(4,128)}) custom-call(bf16[8,128,128]{2,1,0:T(8,128)(2,1)} %stored.1, s32[1,8,8]{2,1,0:T(8,128)} %request.3, s32[4,16]{1,0:T(4,128)} %blocks.3, s32[4]{0:T(128)} %batch_atom.1, f32[3,4,256]{2,1,0:T(4,128)} %offset.3, f32[4,256]{1,0:T(4,128)} %weight.3, f32[3,1000]{1,0:T(4,128)} %xyz.1, ...), custom_call_target="tpu_custom_call" | custom-call | tf_op jit(solution)/shard_map/pallas_call | solution.py:471
  32.6 6.2 %shard_map.113 = (bf16[64,128,128]{2,1,0:T(8,128)(2,1)}, f32[4,1000]{1,0:T(4,128)}, f32[4,256]{1,0:T(4,128)}) custom-call(s32[1,8,8]{2,1,0:T(8,128)} %request.3, s32[4,16]{1,0:T(4,128)} %blocks.3, bf16[4,256,512]{2,1,0:T(8,128)(2,1)} %values.1, f32[32,4,128]{2,1,0:T(4,128)} %get-tuple-element.9.table, f32[4,128]{1,0:T(4,128)} %get-tuple-element.10.own_rows, ...), custom_call_target="tpu_custom_call" | custom-call | tf_op jit(solution)/shard_map/pallas_call | solution.py:508
  38.8 27.6 %shard_map.114 = bf16[8,128,128]{2,1,0:T(8,128)(2,1)} custom-call(bf16[64,128,128]{2,1,0:T(8,128)(2,1)} %get-tuple-element.12.part), custom_call_target="tpu_custom_call" | custom-call | tf_op jit(solution)/shard_map/pallas_call | solution.py:530
  66.4 1.7 %copy.13 = bf16[8,128,128]{2,1,0:T(8,128)(2,1)} copy(bf16[8,128,128]{2,1,0:T(8,128)(2,1)} %shard_map.114) | data formatting | bytes 524288

commit v3 on v2

--- a/solution.py
+++ b/solution.py
@@ -339,16 +339,20 @@
     part,
     result,
     paired,
-    sent_y,
-    came_y,
+    sent_1,
+    came_1,
+    sent_2,
+    came_2,
     outgoing,
     arrived,
     across,
     final,
     send_a,
     recv_a,
-    send_y,
-    recv_y,
+    send_1,
+    recv_1,
+    send_2,
+    recv_2,
     send_b,
     recv_b,
     send_c,
@@ -363,14 +367,17 @@
     quad, lane = g // 4, lax.rem(g, 4)
     core, side = lax.rem(g, 2), lax.rem(g // 2, 2)
     pair, beside = flip(g, 1), flip(g, 2)
+    turn_y, turn_x = 1 - 2 * side, 1 - 2 * lax.rem(me, 2)
+    one = (g + (1 - core) * 2 * turn_y, me + core * turn_x)
+    two = (g + core * 2 * turn_y, me + (1 - core) * turn_x)
 
     peers = [(pair, me), (beside, me)]
-    peers += [(g, flip(me, k)) for k in range(1, devs)]
+    peers += [(g, flip(me, k)) for k in [1, *range(2, devs, 2)]]
     peers += [(lax.rem(quad + j, quads) * 4 + lane, me) for j in range(1, quads)]
     meet(peers)
 
     order = list(range(devs - 1, -1, -1))
-    halves, rows, out = {}, {}, {}
+    halves, first, second, out = {}, {}, {}, {}
     for k in order:
         halves[k] = remote(
             part.at[pl.ds(flip(me, k) * own + (1 - core) * half, half)],
@@ -382,36 +389,68 @@
         )
         halves[k].start()
 
-    def sum_of_pair(k, which):
-        here = part[pl.ds(flip(me, k) * own + core * half + which * quarter, quarter)]
-        there = paired[k, pl.ds(which * quarter, quarter)]
+    def of_pair(a, b, k):
+        over_x = core * a + (1 - core) * b
+        which = side + ((1 - core) * a + core * b) * turn_y
+        row = (flip(me, k) + over_x * turn_x) * own + core * half + which * quarter
+        here = part[pl.ds(row, quarter)]
+        there = paired[k + over_x, pl.ds(which * quarter, quarter)]
         return here.astype(F32) + there.astype(F32)
 
-    def sum_of_four(k):
-        rows[k].wait_recv()
-        return sum_of_pair(k, side) + came_y[k].astype(F32)
-
-    def to_owner(k):
-        outgoing[k] = sum_of_four(k).astype(BF16)
+    def of_four(b, k):
+        first[k + b].wait_recv()
+        return of_pair(0, b, k) + came_1[k + b].astype(F32)
+
+    def of_eight(k):
+        second[k].wait_recv()
+        return of_four(0, k) + came_2[k // 2].astype(F32)
+
+    def step_1(k):
+        halves[k + 1].wait_recv()
+        halves[k].wait_recv()
+        for b in (1, 0):
+            slot = k + b
+            sent_1[slot] = of_pair(1, b, k).astype(BF16)
+            first[slot] = remote(
+                sent_1.at[slot], came_1.at[slot], send_1.at[slot], recv_1.at[slot], *one
+            )
+            first[slot].start()
+
+    def step_2(k):
+        slot = k // 2
+        sent_2[slot] = of_four(1, k).astype(BF16)
+        second[k] = remote(
+            sent_2.at[slot], came_2.at[slot], send_2.at[slot], recv_2.at[slot], *two
+        )
+        second[k].start()
+
+    def step_3(k):
+        slot = k // 2
+        outgoing[slot] = of_eight(k).astype(BF16)
         out[k] = remote(
-            outgoing.at[k], arrived.at[k], send_b.at[k], recv_b.at[k], g, flip(me, k)
+            outgoing.at[slot],
+            arrived.at[slot],
+            send_b.at[slot],
+            recv_b.at[slot],
+            g,
+            flip(me, k),
         )
         out[k].start()
 
-    for step, k in enumerate(order):
-        halves[k].wait_recv()
-        sent_y[k] = sum_of_pair(k, 1 - side).astype(BF16)
-        rows[k] = remote(
-            sent_y.at[k], came_y.at[k], send_y.at[k], recv_y.at[k], beside, me
-        )
-        rows[k].start()
+    planes = list(range(devs - 2, -1, -2))
+    for step, k in enumerate(planes):
+        step_1(k)
+        if step >= 1:
+            step_2(planes[step - 1])
         if step >= 2:
-            to_owner(order[step - 2])
-    to_owner(1)
-    whole = sum_of_four(0)
-    for k in order[:-1]:
+            step_3(planes[step - 2])
+    step_2(0)
+    for k in planes[-2:-1]:
+        step_3(k)
+    whole = of_eight(0)
+    for k in planes[:-1]:
         out[k].wait_recv()
-        whole = whole + arrived[k].astype(F32)
+        whole = whole + arrived[k // 2].astype(F32)
     others = []
     if quads > 1:
         across[quad] = whole.astype(BF16)
@@ -441,7 +480,7 @@
         copy.start()
         copy.wait_recv()
         others.append(copy)
-    for copy in [*halves.values(), *rows.values(), *out.values(), *others]:
+    for copy in [*halves.values(), *first.values(), *second.values(), *out.values(), *others]:
         copy.wait_send()
     result[...] = final[...]
 
@@ -536,10 +575,14 @@
             pltpu.VMEM((devs, half, tile, tile), BF16),
             pltpu.VMEM((devs, quarter, tile, tile), BF16),
             pltpu.VMEM((devs, quarter, tile, tile), BF16),
-            pltpu.VMEM((devs, quarter, tile, tile), BF16),
-            pltpu.VMEM((devs, quarter, tile, tile), BF16),
+            pltpu.VMEM((devs // 2, quarter, tile, tile), BF16),
+            pltpu.VMEM((devs // 2, quarter, tile, tile), BF16),
+            pltpu.VMEM((devs // 2, quarter, tile, tile), BF16),
+            pltpu.VMEM((devs // 2, quarter, tile, tile), BF16),
             pltpu.VMEM((groups // 4, quarter, tile, tile), BF16),
             pltpu.VMEM((own, tile, tile), BF16),
+            dma((devs,)),
+            dma((devs,)),
             dma((devs,)),
             dma((devs,)),
             dma((devs,)),

time: 68.3 us -> 66.7 us (0.977)
  Pallas kernels: 65.8 us -> 64.2 us
    pallas_call x1, Pallas kernels: 27.6 us -> 26 us  [on_device(): pl.pallas_call(functools.partial(reduce_kernel, groups, devs), out_shape=...]
where the time goes in v3:
time: 66.7 us; the launch traced here: 66.5 us
  Pallas kernels  64.2 us (96%)
  local copies, waits for them, and re-layouts  1.67 us (3%)
    pallas_call x1, Pallas kernels, on_device(): pl.pallas_call(functools.partial(density_kernel, groups, devs, capacity),...  31.9 us
    pallas_call x1, Pallas kernels, on_device(): pl.pallas_call(functools.partial(reduce_kernel, groups, devs), out_shape=...  26 us
    pallas_call x1, Pallas kernels, on_device(): pl.pallas_call(functools.partial(term_kernel, capacity, own), out_shape=(...  6.24 us
    unnamed x1, local copies, waits for them, and re-layouts  1.67 us

profile of v3, /device:TPU:0, one launch (start us, length us, event | category | flops | bytes accessed | tf_op | source)
XLA Modules:
  0.0 66.5 jit_solution(17183307516161124424)
XLA Ops:
  0.6 31.9 %shard_map.112 = (f32[4,256]{1,0:T(4,128)}, f32[4,128]{1,0:T(4,128)}, f32[32,4,128]{2,1,0:T(4,128)}) custom-call(bf16[8,128,128]{2,1,0:T(8,128)(2,1)} %stored.1, s32[1,8,8]{2,1,0:T(8,128)} %request.3, s32[4,16]{1,0:T(4,128)} %blocks.3, s32[4]{0:T(128)} %batch_atom.1, f32[3,4,256]{2,1,0:T(4,128)} %offset.3, f32[4,256]{1,0:T(4,128)} %weight.3, f32[3,1000]{1,0:T(4,128)} %xyz.1, ...), custom_call_target="tpu_custom_call" | custom-call | tf_op jit(solution)/shard_map/pallas_call | solution.py:510
  32.6 6.2 %shard_map.113 = (bf16[64,128,128]{2,1,0:T(8,128)(2,1)}, f32[4,1000]{1,0:T(4,128)}, f32[4,256]{1,0:T(4,128)}) custom-call(s32[1,8,8]{2,1,0:T(8,128)} %request.3, s32[4,16]{1,0:T(4,128)} %blocks.3, bf16[4,256,512]{2,1,0:T(8,128)(2,1)} %values.1, f32[32,4,128]{2,1,0:T(4,128)} %get-tuple-element.9.table, f32[4,128]{1,0:T(4,128)} %get-tuple-element.10.own_rows, ...), custom_call_target="tpu_custom_call" | custom-call | tf_op jit(solution)/shard_map/pallas_call | solution.py:547
  38.8 26.0 %shard_map.114 = bf16[8,128,128]{2,1,0:T(8,128)(2,1)} custom-call(bf16[64,128,128]{2,1,0:T(8,128)(2,1)} %get-tuple-element.12.part), custom_call_target="tpu_custom_call" | custom-call | tf_op jit(solution)/shard_map/pallas_call | solution.py:569
  64.8 1.7 %copy.13 = bf16[8,128,128]{2,1,0:T(8,128)(2,1)} copy(bf16[8,128,128]{2,1,0:T(8,128)(2,1)} %shard_map.114) | data formatting | bytes 524288
